TPU v7x, 32 devices: a whole 2x2x4 slice. The times are simulated.
32 devices in a mesh: leaf: 8 (over z, y), grp: 4 (over x, core).
Axes of the slice: x: 2, y: 2, z: 4, core: 2. Of those that a mesh axis runs over, the one named last changes fastest.
Arguments:
- points: bfloat16 [32768, 256], P(('leaf', 'grp')), may hold values from -0.75 to 0.75
- rhs: float32 [32768, 128], P(('leaf', 'grp')), may hold values from -0.8 to 0.8
- permutation: int32 [32768], P(('leaf', 'grp')), may hold values from 0 to 32767, as said below
- leaf_basis: float32 [8192, 1024], P(('leaf', 'grp')), may hold values from -0.1875 to 0.1875
- climb_leaf: float32 [8192, 256], P(('leaf', 'grp')), may hold values from -0.25 to 0.25
- climb_pair: float32 [4096, 256], P(('leaf', 'grp')), may hold values from -0.25 to 0.25
- climb_quad: float32 [2048, 256], P(('leaf', 'grp')), may hold values from -0.25 to 0.25
- skel_points: bfloat16 [1024, 256], P(('leaf', 'grp')), may hold values from -0.75 to 0.75
- near_lists: int32 [32, 8], replicated, may hold values from -1 to 31, as said below
- far_lists: int32 [4, 3], replicated, may hold values from -1 to 3, as said below
Outputs:
- product: float32 [32768, 128], P(('leaf', 'grp'))
Inputs may be any that keep to these rules, and one draw needn't show every extreme that they name: `permutation`: maps each block of 1024 tree positions of one leaf onto the same block of initial indices, each once. `near_lists`: row t starts with t itself, then distinct other leaves of the same aligned block of eight (t // 8), then -1 entries only; some row has 8 leaves. `far_lists`: row m holds one or more distinct nodes other than m first, then -1 entries only; some row has 3 nodes.
All inputs are finite; a program needn't handle non-finite values.
Results may differ from a plain program's by a relative error of at most 0.0003.
Values may be sent and summed in bfloat16 or wider, within the bound.
No kernel may reach another device: no remote copies, remote signals or barrier semaphores. Data moves between devices by JAX's collectives and lax.ppermute only.
A program may use at most 128 MiB of HBM per device.

v0:
```python
import jax
import jax.numpy as jnp
from jax import lax
from jax.sharding import PartitionSpec as P


def partner(value, axis, distance):
    mask = 2**distance
    pairs = [(source, source ^ mask) for source in range(lax.axis_size(axis))]
    return lax.ppermute(value, axis, pairs)


def kernel_block(left, right):
    inner = jnp.dot(left, right.T, preferred_element_type=jnp.float32)
    left_sq = jnp.sum(jnp.square(left.astype(jnp.float32)), axis=1)
    right_sq = jnp.sum(jnp.square(right.astype(jnp.float32)), axis=1)
    product = left_sq[:, None] * right_sq[None, :]
    sine = jnp.sqrt(jnp.maximum(product - inner * inner, 0.0))
    theta = jnp.arctan2(sine, inner)
    return (sine + (jnp.pi - theta) * inner) / jnp.pi


def body(
    points,
    rhs,
    permutation,
    leaf_basis,
    climb_leaf,
    climb_pair,
    climb_quad,
    skel_points,
    near_lists,
    far_lists,
):
    upper_limit = lax.Precision.HIGHEST
    leaf_size = points.shape[0]
    rank = climb_leaf.shape[1]
    width = rhs.shape[1]
    local = permutation % leaf_size
    tree_pts = points[local]
    tree_weight = rhs[local]
    leaf_idx = lax.axis_index("leaf")
    grp_idx = lax.axis_index("grp")
    flat = leaf_idx * lax.axis_size("grp") + grp_idx
    position = flat % 8
    node = flat // 8
    parity = leaf_idx % 2
    skeleton_level_zero = jnp.dot(leaf_basis, tree_weight, precision=upper_limit)
    part_one = jnp.dot(climb_leaf.T, skeleton_level_zero, precision=upper_limit)
    skel_one = part_one + partner(part_one, "grp", 0)
    half = rank // 2
    rows_one = lax.dynamic_slice_in_dim(skel_one, flat % 2 * half, half, 0)
    part_two = jnp.dot(climb_pair.T, rows_one, precision=upper_limit)
    skel_two = lax.psum(part_two, "grp")
    quarter = rank // 4
    rows_two = lax.dynamic_slice_in_dim(skel_two, grp_idx * quarter, quarter, 0)
    part_three = jnp.dot(climb_quad.T, rows_two, precision=upper_limit)
    inner_sum = lax.psum(part_three, "grp")
    skel_three = inner_sum + partner(inner_sum, "leaf", 0)
    eighth = rank // 8
    weight_rows = lax.dynamic_slice_in_dim(skel_three, position * eighth, eighth, 0)
    all_pts = lax.all_gather(skel_points, ("leaf", "grp"), axis=0, tiled=True)
    all_weights = lax.all_gather(weight_rows, ("leaf", "grp"), axis=0, tiled=True)
    own_skel = lax.dynamic_slice_in_dim(all_pts, node * rank, rank, 0)
    far_kernel = kernel_block(own_skel, all_pts)
    col_node = jnp.arange(all_pts.shape[0]) // rank
    far_row = lax.dynamic_slice_in_dim(far_lists, node, 1, 0)[0]
    selected_rows = jnp.any(col_node[:, None] == far_row[None, :], axis=1).astype(jnp.float32)
    up_three = jnp.dot(far_kernel * selected_rows[None, :], all_weights, precision=upper_limit)
    up_two = lax.all_gather(
        jnp.dot(climb_quad, up_three, precision=upper_limit), "grp", axis=0, tiled=True
    )
    mine_half = jnp.dot(climb_pair, up_two, precision=upper_limit)
    other_half = partner(mine_half, "grp", 0)
    up_one = jnp.where(
        flat % 2 == 0,
        jnp.concatenate([mine_half, other_half], 0),
        jnp.concatenate([other_half, mine_half], 0),
    )
    upward_level_zero = jnp.dot(climb_leaf, up_one, precision=upper_limit)
    distant_field = jnp.dot(leaf_basis.T, upward_level_zero, precision=upper_limit)
    four_pts = lax.all_gather(tree_pts, "grp", axis=0, tiled=True)
    four_w = lax.all_gather(tree_weight, "grp", axis=0, tiled=True)
    other_pts = partner(four_pts, "leaf", 0)
    other_w = partner(four_w, "leaf", 0)
    group_pts = jnp.where(
        parity == 0,
        jnp.concatenate([four_pts, other_pts], 0),
        jnp.concatenate([other_pts, four_pts], 0),
    )
    group_w = jnp.where(
        parity == 0, jnp.concatenate([four_w, other_w], 0), jnp.concatenate([other_w, four_w], 0)
    )
    start_leaf = node * 8

    def nearby_block(target, source):
        left = lax.dynamic_slice_in_dim(group_pts, target * leaf_size, leaf_size, 0)
        right = lax.dynamic_slice_in_dim(group_pts, source * leaf_size, leaf_size, 0)
        source_w = lax.dynamic_slice_in_dim(group_w, source * leaf_size, leaf_size, 0)
        return jnp.dot(kernel_block(left, right), source_w, precision=upper_limit)

    group_rows = lax.dynamic_slice_in_dim(near_lists, start_leaf, 8, 0)
    columns = group_rows.shape[1]
    flat_rows = group_rows.reshape(-1)
    valid = flat_rows >= 0
    order_rank = jnp.cumsum(valid.astype(jnp.int32)) - 1
    pairs = jnp.sum(valid.astype(jnp.int32))
    turns = (pairs - position + 7) // 8

    def add_spread(step, totals):
        wanted = position + 8 * step
        slot = jnp.argmax(valid & (order_rank == wanted))
        target = slot // columns
        source = flat_rows[slot] - start_leaf
        return totals.at[target].add(nearby_block(target, source))

    totals = lax.fori_loop(0, turns, add_spread, jnp.zeros((8, leaf_size, width), jnp.float32))
    summed = lax.psum_scatter(
        totals.reshape(2, 4 * leaf_size, width), "grp", scatter_dimension=1, tiled=True
    )
    mine_part = jnp.where(parity == 0, summed[0], summed[1])
    other_part = jnp.where(parity == 0, summed[1], summed[0])
    near = mine_part + partner(other_part, "leaf", 0)
    total = near + distant_field
    return jnp.zeros_like(total).at[local].set(total)


def solution(mesh):
    return jax.shard_map(
        body,
        mesh=mesh,
        in_specs=(
            P(("leaf", "grp"), None),
            P(("leaf", "grp"), None),
            P(("leaf", "grp")),
            P(("leaf", "grp"), None),
            P(("leaf", "grp"), None),
            P(("leaf", "grp"), None),
            P(("leaf", "grp"), None),
            P(("leaf", "grp"), None),
            P(),
            P(),
        ),
        out_specs=P(("leaf", "grp"), None),
        check_vma=False,
    )
```

profile of v0, /device:TPU:0, one launch (start us, length us, event | category | flops | bytes accessed | tf_op | source)
XLA Modules:
  0.0 336.1 jit_solution(18068483424452420095)
XLA Ops:
  6.5 0.8 broadcast_clamp_fusion
  7.4 5.7 %gather_fusion = bf16[1024,256]{1,0:T(8,128)(2,1)} fusion(bf16[1024,256]{1,0:T(8,128)(2,1)} %param.14, s32[1024]{0:T(1024)S(1)} %get-tuple-element.172), kind=kCustom, calls=%fused_computation | custom fusion | bytes 1052672 | tf_op jit(solution)/shard_map/gather | solution.py:40
  13.2 4.0 %gather_fusion.1 = f32[1024,128]{1,0:T(8,128)} fusion(f32[1024,128]{1,0:T(8,128)S(1)} %copy-done.1, s32[1024]{0:T(1024)S(1)} %get-tuple-element.172), kind=kCustom, calls=%fused_computation.1 | custom fusion | bytes 1052672 | tf_op jit(solution)/shard_map/gather | solution.py:41
  17.2 21.3 %all-gather.5.cloned.1.call-done = bf16[4096,256]{1,0:T(8,128)(2,1)} async-done(((bf16[1024,256]{1,0:T(8,128)(2,1)}), bf16[4096,256]{1,0:T(8,128)(2,1)}) %all-gather.5.cloned.1.call-update) | async-done | bytes 2097168 | tf_op jit(solution)/shard_map/all_gather | solution.py:82
  38.6 1.5 collective-permute-start
  40.0 2.7 fusion.79
  42.7 20.0 %all-gather.7.cloned.1.call-done = f32[4096,128]{1,0:T(8,128)} async-done(((f32[1024,128]{1,0:T(8,128)}), f32[4096,128]{1,0:T(8,128)}) %all-gather.7.cloned.1.call-update) | async-done | bytes 2097168 | tf_op jit(solution)/shard_map/all_gather | solution.py:83
  62.7 1.5 collective-permute-start.1
  64.2 1.8 convolution_bitcast_fusion.1
  66.0 0.1 compare_convert_fusion
  66.1 0.6 fusion.78
  67.4 0.1 copy.27
  67.5 0.1 copy.25
  67.5 0.6 reshape.107
  68.1 0.7 reshape.139
  68.8 1.4 reduce-window.9
  70.3 0.6 broadcast_compare_fusion
  70.9 1.8 convolution_bitcast_fusion.3
  72.7 0.9 add_reduce_fusion
  73.6 30.3 %all-reduce.3.cloned.1.call-done = f32[256,128]{0,1:T(8,128)} async-done(((f32[256,128]{0,1:T(8,128)}), f32[256,128]{0,1:T(8,128)}) %all-reduce.3.cloned.1.call-update) | async-done | bytes 131088 | tf_op jit(solution)/shard_map/psum | solution.py:54
  103.9 1.8 convolution_bitcast_fusion.2
  105.8 4.2 %maximum_select_fusion = bf16[8192,256]{1,0:T(8,128)(2,1)} fusion(bf16[4096,256]{1,0:T(8,128)(2,1)} %collective-permute-done, bf16[4096,256]{1,0:T(8,128)(2,1)S(1)} %copy-done.2, pred[]{:T(512)S(6)} %eq.45), kind=kLoop, calls=%fused_computation.36 | loop fusion | flops 18874368 | bytes 8388609 | tf_op jit(solution)/shard_map/jit(_where)/select_n | solution.py:86
  110.1 21.5 %collective-permute-done.1 = f32[4096,128]{1,0:T(8,128)} collective-permute-done((f32[4096,128]{1,0:T(8,128)}, f32[4096,128]{1,0:T(8,128)}, u32[]{:S(2)}, u32[]{:S(2)}) %collective-permute-start.1) | collective-permute-done | bytes 2097184 | tf_op jit(solution)/shard_map/ppermute | solution.py:10
  131.6 4.7 %maximum_select_fusion.1 = f32[8192,128]{1,0:T(8,128)} fusion(f32[4096,128]{1,0:T(8,128)} %collective-permute-done.1, f32[4096,128]{1,0:T(8,128)S(1)} %copy-done.3, pred[]{:T(512)S(6)} %eq.45), kind=kLoop, calls=%fused_computation.37 | loop fusion | flops 3145728 | bytes 8388609 | tf_op jit(solution)/shard_map/jit(_where)/select_n | solution.py:91
  136.3 2.3 broadcast_in_dim.8
  138.6 47.8 %while.13 = (s32[]{:T(128)}, f32[8,1024,128]{2,1,0:T(8,128)}, s32[]{:T(128)}, s32[]{:T(128)}, s32[64]{0:T(128)S(1)}, /*index=5*/pred[64]{0:T(512)(128)(4,1)S(1)}...) while((s32[]{:T(128)}, f32[8,1024,128]{2,1,0:T(8,128)}, ...), condition=%wide.region_7.8_spmd, body=%wide.region_2.0_spmd.sunk | while | flops 2157705728 | bytes 12076940 | solution.py:117
  138.6 0.7 and_reduce_fusion.4
  141.8 0.6 dynamic_slice.87
  144.3 0.7 and_reduce_fusion.5
  145.0 1.5 multiply_reduce_fusion.5
  146.6 1.9 fusion.105
  148.5 14.0 %fusion.106 = f32[8,1024,128]{2,1,0:T(8,128)} fusion(f32[8,1024,128]{2,1,0:T(8,128)} %get-tuple-element.264, s32[]{:T(128)} %select_n.197, f32[1024,1024]{1,0:T(8,128)S(1)} %fusion.105, f32[1024]{0:T(1024)S(1)} %get-tuple-element.240, f32[1024]{0:T(1024)S(1)} %get-tuple-element.241, f32[8192,128]{1,0:T(8,128)} %get-tuple-element.293, ...), kind=kOutput, calls=%fused_computation.22.clone.1 | convolution fusion | flops 1619263488 | bytes 5776388 | tf_op jit(solution)/shard_map/while/body/dot_general | solution.py:100
  162.5 0.7 and_reduce_fusion.4
  165.6 0.6 dynamic_slice.87
  168.1 0.7 and_reduce_fusion.5
  168.9 1.6 multiply_reduce_fusion.5
  170.5 2.0 fusion.105
  172.5 13.9 %fusion.106 = f32[8,1024,128]{2,1,0:T(8,128)} fusion(f32[8,1024,128]{2,1,0:T(8,128)} %get-tuple-element.264, s32[]{:T(128)} %select_n.197, f32[1024,1024]{1,0:T(8,128)S(1)} %fusion.105, f32[1024]{0:T(1024)S(1)} %get-tuple-element.240, f32[1024]{0:T(1024)S(1)} %get-tuple-element.241, f32[8192,128]{1,0:T(8,128)} %get-tuple-element.293, ...), kind=kOutput, calls=%fused_computation.22.clone.1 | convolution fusion | flops 1619263488 | bytes 5776388 | tf_op jit(solution)/shard_map/while/body/dot_general | solution.py:100
  186.4 5.6 %copy.28 = f32[2,4096,128]{1,2,0:T(8,128)} copy(f32[2,4096,128]{2,1,0:T(8,128)} %bitcast.53) | data formatting | bytes 8388608 | tf_op jit(solution)/shard_map/reshape | solution.py:119
  192.1 0.7 copy-done.6
  192.7 57.3 %all_gather.17 = bf16[1024,256]{1,0:T(8,128)(2,1)S(1)} all-gather(bf16[32,256]{1,0:T(8,128)(2,1)S(1)} %copy-done.6), channel_id=1, replica_groups=mesh['leaf'=8,'grp'=4] {'leaf','grp'}, dimensions={0}, use_global_device_ids=true | all-gather | bytes 540672 | tf_op jit(solution)/shard_map/all_gather | solution.py:62
  250.0 0.1 multiply_reduce_fusion.3
  250.1 0.7 fusion.74
  250.8 0.1 compare_reduce_fusion
  250.9 0.3 fusion.62
  251.3 0.1 collective-permute-start.4
  251.4 0.2 multiply_reduce_fusion.2
  251.6 5.7 %collective-permute-done.4 = f32[256,128]{0,1:T(8,128)S(1)} collective-permute-done((f32[256,128]{0,1:T(8,128)}, f32[256,128]{0,1:T(8,128)S(1)}, u32[]{:S(2)}, u32[]{:S(2)}) %collective-permute-start.4) | collective-permute-done | bytes 131104 | tf_op jit(solution)/shard_map/ppermute | solution.py:10
  257.3 0.9 dynamic-slice_add_fusion
  258.2 0.1 copy.29
  258.3 40.2 %all_gather.18 = f32[1024,128]{1,0:T(8,128)S(1)} all-gather(f32[32,128]{1,0:T(8,128)S(1)} %copy.29), channel_id=1, replica_groups=mesh['leaf'=8,'grp'=4] {'leaf','grp'}, dimensions={0}, use_global_device_ids=true | all-gather | bytes 540672 | tf_op jit(solution)/shard_map/all_gather | solution.py:63
  298.5 3.0 fusion.37
  301.6 1.1 convolution_bitcast_fusion.5
  302.7 5.4 %all_gather.19 = f32[256,128]{1,0:T(8,128)S(1)} all-gather(f32[64,128]{1,0:T(8,128)S(1)} %convolution_bitcast_fusion.5), channel_id=1, replica_groups=mesh['leaf'=8,'grp'=4] {'grp'}, dimensions={0}, use_global_device_ids=true | all-gather | bytes 163840 | tf_op jit(solution)/shard_map/all_gather | solution.py:70
  308.1 1.3 select_bitcast_fusion
  309.3 0.1 collective-permute-start.2
  309.4 0.3 convolution_bitcast_fusion.4
  309.7 0.4 collective-permute-start.5
  310.1 0.9 collective-permute-done.5
  311.0 0.4 fusion.56
  311.4 12.2 %collective-permute-done.2 = f32[1024,128]{0,1:T(8,128)S(1)} collective-permute-done((f32[1024,128]{0,1:T(8,128)S(1)}, f32[1024,128]{0,1:T(8,128)S(1)}, u32[]{:S(2)}, u32[]{:S(2)}) %collective-permute-start.2) | collective-permute-done | bytes 524320 | tf_op jit(solution)/shard_map/ppermute | solution.py:10
  323.6 1.9 fusion.48
  325.5 0.2 copy.30
  325.7 3.9 %scatter_custom_fusion = f32[1024,128]{1,0:T(8,128)} fusion(s32[1024]{0:T(1024)S(1)} %get-tuple-element.173, f32[1024,128]{1,0:T(8,128)S(1)} %copy.30, f32[]{:T(128)} %constant.206.clone.1), kind=kCustom, calls=%fused_computation.65 | custom fusion | bytes 524292 | tf_op jit(solution)/shard_map/scatter | solution.py:125
  (36 shorter events, 0.3 us)
Async XLA Ops:
  6.5 33.5 %copy-start = (f32[256,1024]{1,0:T(8,128)S(1)}, f32[256,1024]{1,0:T(8,128)}, u32[]{:S(2)}) copy-start(f32[256,1024]{1,0:T(8,128)} %param.17) | copy-start | bytes 3145732
  6.5 6.6 %copy-start.1 = (f32[1024,128]{1,0:T(8,128)S(1)}, f32[1024,128]{1,0:T(8,128)}, u32[]{:S(2)}) copy-start(f32[1024,128]{1,0:T(8,128)} %param.15) | copy-start | bytes 1572868
  6.5 32.0 %all-gather.5.cloned.1.call-start = ((), (), s32[]{:S(2)}) async-start(), calls=%async_computation.4 | async-start | bytes 2621440 | tf_op jit(solution)/shard_map/all_gather | solution.py:82
  13.1 51.1 %copy-start.4 = (f32[256,256]{1,0:T(8,128)S(1)}, f32[256,256]{1,0:T(8,128)}, u32[]{:S(2)}) copy-start(f32[256,256]{1,0:T(8,128)} %param.18) | copy-start | bytes 786436
  13.1 52.9 %copy-start.8 = (s32[32,8]{0,1:T(8,128)S(1)}, s32[32,8]{0,1:T(8,128)}, u32[]{:S(2)}) copy-start(s32[32,8]{0,1:T(8,128)} %param.22) | copy-start | bytes 3076
  13.1 57.8 %copy-start.5 = (f32[128,256]{1,0:T(8,128)S(1)}, f32[128,256]{1,0:T(8,128)}, u32[]{:S(2)}) copy-start(f32[128,256]{1,0:T(8,128)} %param.19) | copy-start | bytes 393220
  13.1 49.6 %all-gather.7.cloned.1.call-start = ((), (), s32[]{:S(2)}) async-start(), calls=%async_computation.5 | async-start | bytes 2621440 | tf_op jit(solution)/shard_map/all_gather | solution.py:83
  17.2 86.7 %all-reduce.3.cloned.1.call-start = ((), (), s32[]{:S(2)}) async-start(), calls=%async_computation.2 | async-start | bytes 262144 | tf_op jit(solution)/shard_map/psum | solution.py:54
  38.6 67.3 %copy-start.2 = (bf16[4096,256]{1,0:T(8,128)(2,1)S(1)}, bf16[4096,256]{1,0:T(8,128)(2,1)}, u32[]{:S(2)}) copy-start(bf16[4096,256]{1,0:T(8,128)(2,1)} %all-gather.5.cloned.1.call-done) | copy-start | bytes 6291460
  38.6 67.3 %collective-permute-start = (bf16[4096,256]{1,0:T(8,128)(2,1)}, bf16[4096,256]{1,0:T(8,128)(2,1)}, u32[]{:S(2)}, u32[]{:S(2)}) collective-permute-start(bf16[4096,256]{1,0:T(8,128)(2,1)} %all-gather.5.cloned.1.call-done), channel_id=1, source_target_pairs={{0,4},{4,0},{8,12},{12,8},{16,20},{20,16},{24,28},{28,24},{1,5},{5... | collective-permute-start | bytes 6291464 | tf_op jit(solution)/shard_map/ppermute | solution.py:10
  62.7 68.9 %collective-permute-start.1 = (f32[4096,128]{1,0:T(8,128)}, f32[4096,128]{1,0:T(8,128)}, u32[]{:S(2)}, u32[]{:S(2)}) collective-permute-start(f32[4096,128]{1,0:T(8,128)} %all-gather.7.cloned.1.call-done), channel_id=1, source_target_pairs={{0,4},{4,0},{8,12},{12,8},{16,20},{20,16},{24,28},{28,24},{1,5},{5... | collective-permute-start | bytes 6291464 | tf_op jit(solution)/shard_map/ppermute | solution.py:10
  66.0 4.8 %collective-permute-start.3 = (f32[256,128]{0,1:T(8,128)}, f32[256,128]{0,1:T(8,128)}, u32[]{:S(2)}, u32[]{:S(2)}) collective-permute-start(f32[256,128]{0,1:T(8,128)} %convolution_bitcast_fusion.1), channel_id=1, source_target_pairs={{0,1},{1,0},{2,3},{3,2},{4,5},{5,4},{6,7},{7,6},{8,9},{9,8},{10,11... | collective-permute-start | bytes 393224 | tf_op jit(solution)/shard_map/ppermute | solution.py:10
  72.7 178.6 %all-reduce.5.cloned.1.call-start = ((), (), s32[]{:S(2)}) async-start(), calls=%async_computation.3 | async-start | bytes 262144 | tf_op jit(solution)/shard_map/psum | solution.py:58
  105.7 202.3 %reduce-scatter.2.cloned.1.call-start = ((), (), s32[]{:S(2)}) async-start(), calls=%async_computation.1 | async-start | bytes 5242880 | tf_op jit(solution)/shard_map/reduce_scatter | solution.py:118
  105.8 25.8 %copy-start.3 = (f32[4096,128]{1,0:T(8,128)S(1)}, f32[4096,128]{1,0:T(8,128)}, u32[]{:S(2)}) copy-start(f32[4096,128]{1,0:T(8,128)} %all-gather.7.cloned.1.call-done) | copy-start | bytes 6291460
  136.3 2.3 copy-start.7
  136.3 2.3 copy-start.9
  192.0 0.7 copy-start.6
  251.3 6.0 %collective-permute-start.4 = (f32[256,128]{0,1:T(8,128)}, f32[256,128]{0,1:T(8,128)S(1)}, u32[]{:S(2)}, u32[]{:S(2)}) collective-permute-start(f32[256,128]{0,1:T(8,128)} %all-reduce.5.cloned.1.call-done), channel_id=1, source_target_pairs={{0,4},{4,0},{8,12},{12,8},{16,20},{20,16},{24,28},{28,24},{1,5},{5... | collective-permute-start | bytes 393224 | tf_op jit(solution)/shard_map/ppermute | solution.py:10
  309.3 14.2 %collective-permute-start.2 = (f32[1024,128]{0,1:T(8,128)S(1)}, f32[1024,128]{0,1:T(8,128)S(1)}, u32[]{:S(2)}, u32[]{:S(2)}) collective-permute-start(f32[1024,128]{0,1:T(8,128)S(1)} %select_bitcast_fusion), channel_id=1, source_target_pairs={{0,4},{4,0},{8,12},{12,8},{16,20},{20,16},{24,28},{28,24},{1,5},{5... | collective-permute-start | bytes 1572872 | tf_op jit(solution)/shard_map/ppermute | solution.py:10
  309.7 1.3 collective-permute-start.5
Sparse Core Ops, SparseCore 0:
  13.2 25.2 all-gather.4
  40.1 22.5 all-gather.6
  72.8 31.0 all-reduce.2
  106.0 31.7 all-reduce.4
  192.2 67.5 reduce-scatter.1
where the time goes:
time: 337 us; the launch traced here: 336 us
  waiting for transfers between devices  112 us (33%)
  blocking collectives  103 us (31%)
  matrix products  47 us (14%)
  local copies, waits for them, and re-layouts  25.8 us (8%)
  other arithmetic  22 us (7%)
  between operations  14 us (4%)
  loops' own time  8.76 us (3%)
  starting transfers between devices  3.67 us (1%)
    all_gather x1, blocking collectives, body(): all_pts = lax.all_gather(skel_points, ('leaf', 'grp'), axis=0, tiled=True)  57.3 us
    ppermute x6, waiting for transfers between devices, partner(): return lax.ppermute(value, axis, pairs)  40.3 us
    all_gather x1, blocking collectives, body(): lax.all_gather(weight_rows, ('leaf', 'grp'), axis=0, tiled=True)  40.2 us
    psum x1, waiting for transfers between devices, body(): skel_two = lax.psum(part_two, 'grp')  30.3 us
    dot_general x2, matrix products, nearby_block(): return jnp.dot(kernel_block(left, right), source_w, precision=upper_limit)  27.9 us
    all_gather x1, waiting for transfers between devices, body(): four_pts = lax.all_gather(tree_pts, 'grp', axis=0, tiled=True)  21.3 us
    all_gather x1, waiting for transfers between devices, body(): four_w = lax.all_gather(tree_weight, 'grp', axis=0, tiled=True)  20 us
    another operation x1, loops' own time, body(): lax.fori_loop(0, turns, add_spread, jnp.zeros((8, leaf_size, width), jnp....  8.76 us
  transfers between devices with their start and end apart: 11, of which 7 were waited for; matrix products, arithmetic and copies ran while one was open for 24% of the time, Pallas kernels for 0%

commit v1 on v0

--- a/solution.py
+++ b/solution.py
@@ -51,7 +51,10 @@
     half = rank // 2
     rows_one = lax.dynamic_slice_in_dim(skel_one, flat % 2 * half, half, 0)
     part_two = jnp.dot(climb_pair.T, rows_one, precision=upper_limit)
-    skel_two = lax.psum(part_two, "grp")
+    size, skel_two = (lax.axis_size("grp"), part_two)
+    for stride in [1 << k for k in range(size.bit_length() - 1)]:
+        pairs_2 = [(i, i ^ stride) for i in range(size)]
+        skel_two = skel_two + lax.ppermute(skel_two, "grp", pairs_2)
     quarter = rank // 4
     rows_two = lax.dynamic_slice_in_dim(skel_two, grp_idx * quarter, quarter, 0)
     part_three = jnp.dot(climb_quad.T, rows_two, precision=upper_limit)

time: 337 us -> 340 us (level)
    psum x1 -> x0, waiting for transfers between devices: 30.3 us -> none  [body(): skel_two = lax.psum(part_two, 'grp')]
    ppermute x6, waiting for transfers between devices: 40.3 us -> 68.2 us  [partner(): return lax.ppermute(value, axis, pairs)]
  transfers between devices with their start and end apart: 11 -> 12, of which waited for: 7 -> 10; matrix products, arithmetic and copies ran while one was open for 24% -> 24% of each run, Pallas kernels for 0% -> 0%
where the time goes in v1:
time: 340 us; the launch traced here: 339 us
  waiting for transfers between devices  111 us (33%)
  blocking collectives  104 us (31%)
  matrix products  46.5 us (14%)
  local copies, waits for them, and re-layouts  25.9 us (8%)
  other arithmetic  23.6 us (7%)
  between operations  14 us (4%)
  loops' own time  9.64 us (3%)
  starting transfers between devices  4.41 us (1%)
    ppermute x6, waiting for transfers between devices, partner(): return lax.ppermute(value, axis, pairs)  68.2 us
    all_gather x1, blocking collectives, body(): all_pts = lax.all_gather(skel_points, ('leaf', 'grp'), axis=0, tiled=True)  58 us
    all_gather x1, blocking collectives, body(): lax.all_gather(weight_rows, ('leaf', 'grp'), axis=0, tiled=True)  40.1 us
    dot_general x2, matrix products, nearby_block(): return jnp.dot(kernel_block(left, right), source_w, precision=upper_limit)  28 us
    all_gather x1, waiting for transfers between devices, body(): four_pts = lax.all_gather(tree_pts, 'grp', axis=0, tiled=True)  21.3 us
    all_gather x1, waiting for transfers between devices, body(): four_w = lax.all_gather(tree_weight, 'grp', axis=0, tiled=True)  20 us
    another operation x1, loops' own time, body(): lax.fori_loop(0, turns, add_spread, jnp.zeros((8, leaf_size, width), jnp....  9.64 us
  transfers between devices with their start and end apart: 12, of which 10 were waited for; matrix products, arithmetic and copies ran while one was open for 24% of the time, Pallas kernels for 0%

profile of v1, /device:TPU:0, one launch (start us, length us, event | category | flops | bytes accessed | tf_op | source)
XLA Modules:
  0.0 338.5 jit_solution(14581231371489984871)
XLA Ops:
  6.5 1.4 broadcast_clamp_fusion
  8.0 5.7 %gather_fusion = bf16[1024,256]{1,0:T(8,128)(2,1)} fusion(bf16[1024,256]{1,0:T(8,128)(2,1)} %param.14, s32[1024]{0:T(1024)S(1)} %get-tuple-element.172), kind=kCustom, calls=%fused_computation | custom fusion | bytes 1052672 | tf_op jit(solution)/shard_map/gather | solution.py:40
  13.8 4.0 %gather_fusion.1 = f32[1024,128]{1,0:T(8,128)} fusion(f32[1024,128]{1,0:T(8,128)S(1)} %copy-done.1, s32[1024]{0:T(1024)S(1)} %get-tuple-element.172), kind=kCustom, calls=%fused_computation.1 | custom fusion | bytes 1052672 | tf_op jit(solution)/shard_map/gather | solution.py:41
  17.8 21.3 %all-gather.5.cloned.1.call-done = bf16[4096,256]{1,0:T(8,128)(2,1)} async-done(((bf16[1024,256]{1,0:T(8,128)(2,1)}), bf16[4096,256]{1,0:T(8,128)(2,1)}) %all-gather.5.cloned.1.call-update) | async-done | bytes 2097168 | tf_op jit(solution)/shard_map/all_gather | solution.py:85
  39.1 1.5 collective-permute-start
  40.6 2.7 fusion.79
  43.3 20.0 %all-gather.7.cloned.1.call-done = f32[4096,128]{1,0:T(8,128)} async-done(((f32[1024,128]{1,0:T(8,128)}), f32[4096,128]{1,0:T(8,128)}) %all-gather.7.cloned.1.call-update) | async-done | bytes 2097168 | tf_op jit(solution)/shard_map/all_gather | solution.py:86
  63.3 1.5 collective-permute-start.1
  64.8 1.8 convolution_bitcast_fusion.1
  66.8 0.7 reshape.107
  67.4 0.9 collective-permute-done.3
  68.3 1.1 convolution_bitcast_fusion.3
  69.4 0.2 collective-permute-start.4
  69.7 0.7 broadcast_compare_fusion
  70.3 0.5 collective-permute-done.4
  70.9 0.7 add.151
  71.5 0.6 collective-permute-start.5
  72.1 0.7 fusion.78
  73.5 0.7 reshape.139
  74.2 1.4 reduce-window.9
  75.6 0.9 add_reduce_fusion
  76.5 0.9 collective-permute-done.5
  77.4 1.9 convolution_bitcast_fusion.2
  79.3 8.6 %collective-permute-done = bf16[4096,256]{1,0:T(8,128)(2,1)} collective-permute-done((bf16[4096,256]{1,0:T(8,128)(2,1)}, bf16[4096,256]{1,0:T(8,128)(2,1)}, u32[]{:S(2)}, u32[]{:S(2)}) %collective-permute-start) | collective-permute-done | bytes 2097184 | tf_op jit(solution)/shard_map/ppermute | solution.py:10
  88.0 4.2 %maximum_select_fusion = bf16[8192,256]{1,0:T(8,128)(2,1)} fusion(bf16[4096,256]{1,0:T(8,128)(2,1)} %collective-permute-done, bf16[4096,256]{1,0:T(8,128)(2,1)S(1)} %copy-done.2, pred[]{:T(512)S(6)} %eq.45), kind=kLoop, calls=%fused_computation.36 | loop fusion | flops 18874368 | bytes 8388609 | tf_op jit(solution)/shard_map/jit(_where)/select_n | solution.py:89
  92.2 40.0 %collective-permute-done.1 = f32[4096,128]{1,0:T(8,128)} collective-permute-done((f32[4096,128]{1,0:T(8,128)}, f32[4096,128]{1,0:T(8,128)}, u32[]{:S(2)}, u32[]{:S(2)}) %collective-permute-start.1) | collective-permute-done | bytes 2097184 | tf_op jit(solution)/shard_map/ppermute | solution.py:10
  132.2 4.7 %maximum_select_fusion.1 = f32[8192,128]{1,0:T(8,128)} fusion(f32[4096,128]{1,0:T(8,128)} %collective-permute-done.1, f32[4096,128]{1,0:T(8,128)S(1)} %copy-done.3, pred[]{:T(512)S(6)} %eq.45), kind=kLoop, calls=%fused_computation.37 | loop fusion | flops 3145728 | bytes 8388609 | tf_op jit(solution)/shard_map/jit(_where)/select_n | solution.py:94
  136.9 2.3 broadcast_in_dim.8
  139.2 48.9 %while.13 = (s32[]{:T(128)}, f32[8,1024,128]{2,1,0:T(8,128)}, s32[]{:T(128)}, s32[]{:T(128)}, s32[64]{0:T(128)S(1)}, /*index=5*/pred[64]{0:T(512)(128)(4,1)S(1)}...) while((s32[]{:T(128)}, f32[8,1024,128]{2,1,0:T(8,128)}, ...), condition=%wide.region_7.8_spmd, body=%wide.region_2.0_spmd.sunk | while | flops 2157705728 | bytes 12076940 | solution.py:120
  139.2 0.7 and_reduce_fusion.4
  142.7 0.6 dynamic_slice.93
  145.3 0.8 and_reduce_fusion.5
  146.1 1.5 multiply_reduce_fusion.5
  147.7 1.9 fusion.105
  149.6 14.0 %fusion.106 = f32[8,1024,128]{2,1,0:T(8,128)} fusion(f32[8,1024,128]{2,1,0:T(8,128)} %get-tuple-element.265, s32[]{:T(128)} %select_n.197, f32[1024,1024]{1,0:T(8,128)S(1)} %fusion.105, f32[1024]{0:T(1024)S(1)} %get-tuple-element.241, f32[1024]{0:T(1024)S(1)} %get-tuple-element.242, f32[8192,128]{1,0:T(8,128)} %get-tuple-element.294, ...), kind=kOutput, calls=%fused_computation.22.clone.1 | convolution fusion | flops 1619263488 | bytes 5776388 | tf_op jit(solution)/shard_map/while/body/dot_general | solution.py:103
  163.7 0.7 and_reduce_fusion.4
  167.1 0.6 dynamic_slice.93
  169.8 0.8 and_reduce_fusion.5
  170.6 1.6 multiply_reduce_fusion.5
  172.2 2.0 fusion.105
  174.1 14.0 %fusion.106 = f32[8,1024,128]{2,1,0:T(8,128)} fusion(f32[8,1024,128]{2,1,0:T(8,128)} %get-tuple-element.265, s32[]{:T(128)} %select_n.197, f32[1024,1024]{1,0:T(8,128)S(1)} %fusion.105, f32[1024]{0:T(1024)S(1)} %get-tuple-element.241, f32[1024]{0:T(1024)S(1)} %get-tuple-element.242, f32[8192,128]{1,0:T(8,128)} %get-tuple-element.294, ...), kind=kOutput, calls=%fused_computation.22.clone.1 | convolution fusion | flops 1619263488 | bytes 5776388 | tf_op jit(solution)/shard_map/while/body/dot_general | solution.py:103
  188.1 5.6 %copy.28 = f32[2,4096,128]{1,2,0:T(8,128)} copy(f32[2,4096,128]{2,1,0:T(8,128)} %bitcast.53) | data formatting | bytes 8388608 | tf_op jit(solution)/shard_map/reshape | solution.py:122
  193.8 0.7 copy-done.6
  194.5 58.0 %all_gather.17 = bf16[1024,256]{1,0:T(8,128)(2,1)S(1)} all-gather(bf16[32,256]{1,0:T(8,128)(2,1)S(1)} %copy-done.6), channel_id=1, replica_groups=mesh['leaf'=8,'grp'=4] {'leaf','grp'}, dimensions={0}, use_global_device_ids=true | all-gather | bytes 540672 | tf_op jit(solution)/shard_map/all_gather | solution.py:65
  252.4 0.1 multiply_reduce_fusion.3
  252.5 0.7 fusion.74
  253.2 0.1 compare_reduce_fusion
  253.3 0.3 fusion.62
  253.8 0.2 multiply_reduce_fusion.2
  254.0 5.7 %collective-permute-done.6 = f32[256,128]{0,1:T(8,128)S(1)} collective-permute-done((f32[256,128]{0,1:T(8,128)}, f32[256,128]{0,1:T(8,128)S(1)}, u32[]{:S(2)}, u32[]{:S(2)}) %collective-permute-start.6) | collective-permute-done | bytes 131104 | tf_op jit(solution)/shard_map/ppermute | solution.py:10
  259.7 0.9 dynamic-slice_add_fusion
  260.7 40.1 %all_gather.18 = f32[1024,128]{1,0:T(8,128)S(1)} all-gather(f32[32,128]{1,0:T(8,128)S(1)} %copy.29), channel_id=1, replica_groups=mesh['leaf'=8,'grp'=4] {'leaf','grp'}, dimensions={0}, use_global_device_ids=true | all-gather | bytes 540672 | tf_op jit(solution)/shard_map/all_gather | solution.py:66
  300.9 3.0 fusion.37
  303.9 1.1 convolution_bitcast_fusion.5
  305.0 5.4 %all_gather.19 = f32[256,128]{1,0:T(8,128)S(1)} all-gather(f32[64,128]{1,0:T(8,128)S(1)} %convolution_bitcast_fusion.5), channel_id=1, replica_groups=mesh['leaf'=8,'grp'=4] {'grp'}, dimensions={0}, use_global_device_ids=true | all-gather | bytes 163840 | tf_op jit(solution)/shard_map/all_gather | solution.py:73
  310.4 1.3 select_bitcast_fusion
  311.7 0.3 convolution_bitcast_fusion.4
  312.0 0.4 collective-permute-start.7
  312.4 0.9 collective-permute-done.7
  313.3 0.4 fusion.56
  313.7 12.2 %collective-permute-done.2 = f32[1024,128]{0,1:T(8,128)S(1)} collective-permute-done((f32[1024,128]{0,1:T(8,128)S(1)}, f32[1024,128]{0,1:T(8,128)S(1)}, u32[]{:S(2)}, u32[]{:S(2)}) %collective-permute-start.2) | collective-permute-done | bytes 524320 | tf_op jit(solution)/shard_map/ppermute | solution.py:10
  325.9 1.9 fusion.48
  327.8 0.2 copy.30
  328.0 4.0 %scatter_custom_fusion = f32[1024,128]{1,0:T(8,128)} fusion(s32[1024]{0:T(1024)} %get-tuple-element.173, f32[1024,128]{1,0:T(8,128)S(1)} %copy.30, f32[]{:T(128)} %constant.206.clone.1), kind=kCustom, calls=%fused_computation.65 | custom fusion | bytes 524800 | tf_op jit(solution)/shard_map/scatter | solution.py:128
  (37 shorter events, 0.7 us)
Async XLA Ops:
  6.5 34.1 %copy-start = (f32[256,1024]{1,0:T(8,128)S(1)}, f32[256,1024]{1,0:T(8,128)}, u32[]{:S(2)}) copy-start(f32[256,1024]{1,0:T(8,128)} %param.17) | copy-start | bytes 3145732
  6.5 7.2 %copy-start.1 = (f32[1024,128]{1,0:T(8,128)S(1)}, f32[1024,128]{1,0:T(8,128)}, u32[]{:S(2)}) copy-start(f32[1024,128]{1,0:T(8,128)} %param.15) | copy-start | bytes 1572868
  6.5 32.6 %all-gather.5.cloned.1.call-start = ((), (), s32[]{:S(2)}) async-start(), calls=%async_computation.3 | async-start | bytes 2621440 | tf_op jit(solution)/shard_map/all_gather | solution.py:85
  13.7 51.1 %copy-start.4 = (f32[256,256]{1,0:T(8,128)S(1)}, f32[256,256]{1,0:T(8,128)}, u32[]{:S(2)}) copy-start(f32[256,256]{1,0:T(8,128)} %param.18) | copy-start | bytes 786436
  13.7 52.9 %copy-start.8 = (s32[32,8]{0,1:T(8,128)S(1)}, s32[32,8]{0,1:T(8,128)}, u32[]{:S(2)}) copy-start(s32[32,8]{0,1:T(8,128)} %param.22) | copy-start | bytes 3076
  13.7 54.6 %copy-start.5 = (f32[128,256]{1,0:T(8,128)S(1)}, f32[128,256]{1,0:T(8,128)}, u32[]{:S(2)}) copy-start(f32[128,256]{1,0:T(8,128)} %param.19) | copy-start | bytes 393220
  13.7 49.6 %all-gather.7.cloned.1.call-start = ((), (), s32[]{:S(2)}) async-start(), calls=%async_computation.4 | async-start | bytes 2621440 | tf_op jit(solution)/shard_map/all_gather | solution.py:86
  17.8 235.9 %all-reduce.2.cloned.1.call-start = ((), (), s32[]{:S(2)}) async-start(), calls=%async_computation.2 | async-start | bytes 262144 | tf_op jit(solution)/shard_map/psum | solution.py:61
  39.1 48.8 %copy-start.2 = (bf16[4096,256]{1,0:T(8,128)(2,1)S(1)}, bf16[4096,256]{1,0:T(8,128)(2,1)}, u32[]{:S(2)}) copy-start(bf16[4096,256]{1,0:T(8,128)(2,1)} %all-gather.5.cloned.1.call-done) | copy-start | bytes 6291460
  39.1 48.8 %collective-permute-start = (bf16[4096,256]{1,0:T(8,128)(2,1)}, bf16[4096,256]{1,0:T(8,128)(2,1)}, u32[]{:S(2)}, u32[]{:S(2)}) collective-permute-start(bf16[4096,256]{1,0:T(8,128)(2,1)} %all-gather.5.cloned.1.call-done), channel_id=1, source_target_pairs={{0,4},{4,0},{8,12},{12,8},{16,20},{20,16},{24,28},{28,24},{1,5},{5... | collective-permute-start | bytes 6291464 | tf_op jit(solution)/shard_map/ppermute | solution.py:10
  63.3 68.9 %collective-permute-start.1 = (f32[4096,128]{1,0:T(8,128)}, f32[4096,128]{1,0:T(8,128)}, u32[]{:S(2)}, u32[]{:S(2)}) collective-permute-start(f32[4096,128]{1,0:T(8,128)} %all-gather.7.cloned.1.call-done), channel_id=1, source_target_pairs={{0,4},{4,0},{8,12},{12,8},{16,20},{20,16},{24,28},{28,24},{1,5},{5... | collective-permute-start | bytes 6291464 | tf_op jit(solution)/shard_map/ppermute | solution.py:10
  66.6 1.7 collective-permute-start.3
  69.4 1.4 collective-permute-start.4
  71.5 5.9 %collective-permute-start.5 = (f32[256,128]{0,1:T(8,128)}, f32[256,128]{0,1:T(8,128)}, u32[]{:S(2)}, u32[]{:S(2)}) collective-permute-start(f32[256,128]{0,1:T(8,128)} %add.151), channel_id=1, source_target_pairs={{0,2},{1,3},{2,0},{3,1},{4,6},{5,7},{6,4},{7,5},{8,10},{9,11},{10,... | collective-permute-start | bytes 393224 | tf_op jit(solution)/shard_map/ppermute | solution.py:57
  79.3 231.1 %reduce-scatter.2.cloned.1.call-start = ((), (), s32[]{:S(2)}) async-start(), calls=%async_computation.1 | async-start | bytes 5242880 | tf_op jit(solution)/shard_map/reduce_scatter | solution.py:121
  79.3 52.8 %copy-start.3 = (f32[4096,128]{1,0:T(8,128)S(1)}, f32[4096,128]{1,0:T(8,128)}, u32[]{:S(2)}) copy-start(f32[4096,128]{1,0:T(8,128)} %all-gather.7.cloned.1.call-done) | copy-start | bytes 6291460
  136.9 2.3 copy-start.7
  136.9 2.3 copy-start.9
  193.7 0.7 copy-start.6
  253.7 6.0 %collective-permute-start.6 = (f32[256,128]{0,1:T(8,128)}, f32[256,128]{0,1:T(8,128)S(1)}, u32[]{:S(2)}, u32[]{:S(2)}) collective-permute-start(f32[256,128]{0,1:T(8,128)} %all-reduce.2.cloned.1.call-done), channel_id=1, source_target_pairs={{0,4},{4,0},{8,12},{12,8},{16,20},{20,16},{24,28},{28,24},{1,5},{5... | collective-permute-start | bytes 393224 | tf_op jit(solution)/shard_map/ppermute | solution.py:10
  311.6 14.2 %collective-permute-start.2 = (f32[1024,128]{0,1:T(8,128)S(1)}, f32[1024,128]{0,1:T(8,128)S(1)}, u32[]{:S(2)}, u32[]{:S(2)}) collective-permute-start(f32[1024,128]{0,1:T(8,128)S(1)} %select_bitcast_fusion), channel_id=1, source_target_pairs={{0,4},{4,0},{8,12},{12,8},{16,20},{20,16},{24,28},{28,24},{1,5},{5... | collective-permute-start | bytes 1572872 | tf_op jit(solution)/shard_map/ppermute | solution.py:10
  312.0 1.3 collective-permute-start.7
Sparse Core Ops, SparseCore 0:
  13.8 25.2 all-gather.4
  40.7 22.5 all-gather.6
  79.4 30.8 all-reduce.1
  193.9 68.1 reduce-scatter.1
